TPU v7x, 32 devices: a whole 2x2x4 slice. The times are simulated.
32 devices in a mesh: dom: 32 (over z, y, x, core).
Axes of the slice: x: 2, y: 2, z: 4, core: 2. Of those that a mesh axis runs over, the one named last changes fastest.
Arguments:
- start_point: float32 [16384, 128], P('dom'), may hold values from -6 to 6
- residual: float32 [16384, 128], P('dom'), may hold values from -40 to 40
- direction: float32 [16384, 128], P('dom'), may hold values from -40 to 40
- send_list: int32 [32, 4, 3], P('dom'), may hold values from 0 to 3, as said below
- block_cols: int32 [128, 6], P('dom'), may hold values from 0 to 15, as said below
- block_vals: float32 [128, 6, 128, 128], P('dom'), may hold values from -0.2 to 8.1, as said below
Outputs:
- new_point: float32 [16384, 128], P('dom')
- new_residual: float32 [16384, 128], P('dom')
- new_direction: float32 [16384, 128], P('dom')
Inputs may be any that keep to these rules, and one draw needn't show every extreme that they name: send_list[t, m] lists, in its first entries, the distinct blocks of partition t that the partition at offset -off (off as in the first step) reads; between 1 and 3 of them are read for each pair, and some pair reads 3; the other entries are valid block numbers that are never read. `block_cols`: entry 0 of a block row names the row's own block; a block that couples two partitions appears in both partitions' rows, transposed; the assembled matrix is symmetric positive definite. `block_vals`: stored blocks that no coupling uses are zero.
All inputs are finite; a program needn't handle non-finite values.
Results may differ from a plain program's by a relative error of at most 0.0003.
Values sent between devices are 32-bit elements; how exact they have to be, the bound alone decides.
No kernel may reach another device: no remote copies, remote signals or barrier semaphores. Data moves between devices by JAX's collectives and lax.ppermute only.
A program may use at most 128 MiB of HBM per device.

v0:
```python
import jax
import jax.numpy as jnp
from jax import lax
from jax.sharding import PartitionSpec as P

STEPS = 6
BASIS = 13
center_value = 4.5
half_range = 4.5


def from_behind(shard, axis, by):
    peers = lax.axis_size(axis)
    return lax.ppermute(shard, axis, [(i, (i + by) % peers) for i in range(peers)])


def apply_blocks(blocked, send_rows, block_cols, block_vals):
    block_count, block_rows, width = blocked.shape
    highest = lax.Precision.HIGHEST
    flat_rows = blocked.reshape(block_count, block_rows * width)
    hop_count = send_rows.shape[0] // 2
    own_ids = jnp.arange(block_count, dtype=jnp.int32)
    pieces = [flat_rows]
    for slot_index in range(2 * hop_count):
        offset = slot_index + 1 if slot_index < hop_count else hop_count - 1 - slot_index
        chooser = (send_rows[slot_index][:, None] == own_ids[None, :]).astype(jnp.float32)
        outgoing = jnp.dot(chooser, flat_rows, precision=highest)
        pieces.append(from_behind(outgoing, "dom", -offset))
    ghost_table = jnp.concatenate(pieces, axis=0)
    ghost_ids = jnp.arange(ghost_table.shape[0], dtype=jnp.int32)
    running = jnp.zeros((block_count, block_rows, width), jnp.float32)
    for slot_index in range(block_cols.shape[1]):
        chooser = (block_cols[:, slot_index][:, None] == ghost_ids[None, :]).astype(jnp.float32)
        picked = jnp.dot(chooser, ghost_table, precision=highest).reshape(
            block_count, block_rows, width
        )
        running = running + jnp.einsum(
            "icb,ibw->icw", block_vals[:, slot_index], picked, precision=highest
        )
    return running


def next_vector(vector, send_rows, block_cols, block_vals):
    block_count = block_vals.shape[0]
    block_rows = block_vals.shape[2]
    blocked = vector.reshape(block_count, block_rows, vector.shape[1])
    image_part = apply_blocks(blocked, send_rows, block_cols, block_vals).reshape(vector.shape)
    return (image_part - center_value * vector) / half_range


def basis_change():
    positions = jnp.arange(BASIS)
    row_ids = positions[:, None]
    col_ids = positions[None, :]
    active = (col_ids < STEPS) | (col_ids > STEPS) & (col_ids < BASIS - 1)
    change_table = jnp.where(active & (row_ids == col_ids), center_value, 0.0)
    change_table = change_table + jnp.where(active & (row_ids == col_ids + 1), half_range, 0.0)
    return change_table.astype(jnp.float32)


def coefficient_steps(gram_matrix):
    change_table = basis_change()
    column_count = gram_matrix.shape[0]
    positions = jnp.arange(BASIS)
    point_c = jnp.zeros((column_count, BASIS), jnp.float32)
    resid_c = jnp.broadcast_to((positions == STEPS + 1).astype(jnp.float32), (column_count, BASIS))
    direc_c = jnp.broadcast_to((positions == 0).astype(jnp.float32), (column_count, BASIS))
    highest = lax.Precision.HIGHEST
    for step_index in range(STEPS):
        current = jnp.sum(
            resid_c * jnp.einsum("nab,nb->na", gram_matrix, resid_c, precision=highest), axis=1
        )
        moved_dir = jnp.einsum("ab,nb->na", change_table, direc_c, precision=highest)
        curvature = jnp.sum(
            direc_c * jnp.einsum("nab,nb->na", gram_matrix, moved_dir, precision=highest), axis=1
        )
        alpha_step = current / curvature
        point_c = point_c + alpha_step[:, None] * direc_c
        resid_c = resid_c - alpha_step[:, None] * moved_dir
        following = jnp.sum(
            resid_c * jnp.einsum("nab,nb->na", gram_matrix, resid_c, precision=highest), axis=1
        )
        direc_c = resid_c + (following / current)[:, None] * direc_c
    return (point_c, resid_c, direc_c)


def shards(start_point, residual, direction, send_list, block_cols, block_vals):
    send_rows = send_list[0]
    p_basis = [direction]
    r_basis = [residual]
    for power_step in range(STEPS):
        p_basis.append(next_vector(p_basis[-1], send_rows, block_cols, block_vals))
    for power_step in range(STEPS - 1):
        r_basis.append(next_vector(r_basis[-1], send_rows, block_cols, block_vals))
    basis_stack = jnp.stack(p_basis + r_basis)
    local_gram = jnp.einsum(
        "arn,brn->nab", basis_stack, basis_stack, precision=lax.Precision.HIGHEST
    )
    gram_matrix = lax.psum(local_gram, "dom")
    point_c, resid_c, direc_c = coefficient_steps(gram_matrix)
    highest = lax.Precision.HIGHEST
    new_point = start_point + jnp.einsum("na,arn->rn", point_c, basis_stack, precision=highest)
    new_residual = jnp.einsum("na,arn->rn", resid_c, basis_stack, precision=highest)
    new_direction = jnp.einsum("na,arn->rn", direc_c, basis_stack, precision=highest)
    return (new_point, new_residual, new_direction)


def solution(mesh):
    return jax.shard_map(
        shards,
        mesh=mesh,
        in_specs=(
            P("dom", None),
            P("dom", None),
            P("dom", None),
            P("dom", None, None),
            P("dom", None),
            P("dom", None, None, None),
        ),
        out_specs=(P("dom", None), P("dom", None), P("dom", None)),
        check_vma=False,
    )
```

profile of v0, /device:TPU:0, one launch (start us, length us, event | category | flops | bytes accessed | tf_op | source)
XLA Modules:
  0.0 516.2 jit_solution(13102410080200635533)
XLA Ops:
  9.9 6.5 %collective-permute-start.24 = (f32[3,16384]{1,0:T(4,128)S(1)}, f32[3,16384]{1,0:T(4,128)S(1)}, u32[]{:S(2)}, u32[]{:S(2)}) collective-permute-start(f32[3,16384]{1,0:T(4,128)S(1)} %fusion.361), channel_id=1, source_target_pairs={{0,31},{1,0},{2,1},{3,2},{4,3},{5,4},{6,5},{7,6},{8,7},{9,8},{10,9... | collective-permute-start | bytes 589832 | tf_op jit(solution)/shard_map/ppermute | solution.py:14
  21.1 5.0 collective-permute-start
  32.6 7.7 %collective-permute-start.3 = (f32[3,16384]{1,0:T(4,128)}, f32[3,16384]{1,0:T(4,128)}, u32[]{:S(2)}, u32[]{:S(2)}) collective-permute-start(f32[3,16384]{1,0:T(4,128)} %fusion.334), channel_id=1, source_target_pairs={{0,2},{1,3},{2,4},{3,5},{4,6},{5,7},{6,8},{7,9},{8,10},{9,11},{10,... | collective-permute-start | bytes 589832 | tf_op jit(solution)/shard_map/ppermute | solution.py:14
  53.3 6.4 %concatenate.33 = f32[16,16384]{1,0:T(8,128)S(1)} concatenate(f32[4,16384]{1,0:T(4,128)S(1)} %reshape_reshape.33, f32[3,16384]{1,0:T(4,128)} %collective-permute-done, f32[3,16384]{1,0:T(4,128)} %collective-permute-done.1, f32[3,16384]{1,0:T(4,128)} %collective-permute-done.2, f32[3,16384]{1,0:T(4,128)} %collective-permute-done.3), dimensions={0} | concatenate | bytes 2097152 | tf_op jit(solution)/shard_map/concatenate | solution.py:29
  73.6 5.0 collective-permute-start.4
  83.7 12.6 %collective-permute-start.7 = (f32[3,16384]{1,0:T(4,128)}, f32[3,16384]{1,0:T(4,128)}, u32[]{:S(2)}, u32[]{:S(2)}) collective-permute-start(f32[3,16384]{1,0:T(4,128)} %fusion.333), channel_id=1, source_target_pairs={{0,2},{1,3},{2,4},{3,5},{4,6},{5,7},{6,8},{7,9},{8,10},{9,11},{10,... | collective-permute-start | bytes 589832 | tf_op jit(solution)/shard_map/ppermute | solution.py:14
  96.2 6.5 %concatenate.40 = f32[16,16384]{1,0:T(8,128)S(1)} concatenate(f32[4,16384]{1,0:T(4,128)S(1)} %reshape_reshape.40, f32[3,16384]{1,0:T(4,128)} %copy-done.37, f32[3,16384]{1,0:T(4,128)} %copy-done.40, f32[3,16384]{1,0:T(4,128)} %copy-done.43, f32[3,16384]{1,0:T(4,128)} %collective-permute-done.31), dimensions={0} | concatenate | bytes 2097152 | tf_op jit(solution)/shard_map/concatenate | solution.py:29
  113.2 6.7 %concatenate.34 = f32[16,16384]{1,0:T(8,128)S(1)} concatenate(f32[4,16384]{1,0:T(4,128)S(1)} %reshape_reshape.34, f32[3,16384]{1,0:T(4,128)} %collective-permute-done.4, f32[3,16384]{1,0:T(4,128)} %collective-permute-done.5, f32[3,16384]{1,0:T(4,128)} %collective-permute-done.6, f32[3,16384]{1,0:T(4,128)} %collective-permute-done.7), dimensions={0} | concatenate | bytes 2097152 | tf_op jit(solution)/shard_map/concatenate | solution.py:29
  132.9 4.6 collective-permute-start.32
  140.8 10.1 %collective-permute-start.9 = (f32[3,16384]{1,0:T(4,128)}, f32[3,16384]{1,0:T(4,128)}, u32[]{:S(2)}, u32[]{:S(2)}) collective-permute-start(f32[3,16384]{1,0:T(4,128)} %fusion.354), channel_id=1, source_target_pairs={{0,30},{1,31},{2,0},{3,1},{4,2},{5,3},{6,4},{7,5},{8,6},{9,7},{10,... | collective-permute-start | bytes 589832 | tf_op jit(solution)/shard_map/ppermute | solution.py:14
  151.0 5.4 %collective-permute-start.8 = (f32[3,16384]{1,0:T(4,128)}, f32[3,16384]{1,0:T(4,128)}, u32[]{:S(2)}, u32[]{:S(2)}) collective-permute-start(f32[3,16384]{1,0:T(4,128)} %fusion.365), channel_id=1, source_target_pairs={{0,31},{1,0},{2,1},{3,2},{4,3},{5,4},{6,5},{7,6},{8,7},{9,8},{10,9... | collective-permute-start | bytes 589832 | tf_op jit(solution)/shard_map/ppermute | solution.py:14
  170.9 6.4 %concatenate.35 = f32[16,16384]{1,0:T(8,128)S(1)} concatenate(f32[4,16384]{1,0:T(4,128)S(1)} %reshape_reshape.35, f32[3,16384]{1,0:T(4,128)} %collective-permute-done.8, f32[3,16384]{1,0:T(4,128)} %collective-permute-done.9, f32[3,16384]{1,0:T(4,128)} %collective-permute-done.10, f32[3,16384]{1,0:T(4,128)} %collective-permute-done.11), dimensions={0} | concatenate | bytes 2097152 | tf_op jit(solution)/shard_map/concatenate | solution.py:29
  206.1 6.6 %collective-permute-start.15 = (f32[3,16384]{1,0:T(4,128)}, f32[3,16384]{1,0:T(4,128)}, u32[]{:S(2)}, u32[]{:S(2)}) collective-permute-start(f32[3,16384]{1,0:T(4,128)} %fusion.331), channel_id=1, source_target_pairs={{0,2},{1,3},{2,4},{3,5},{4,6},{5,7},{6,8},{7,9},{8,10},{9,11},{10,... | collective-permute-start | bytes 589832 | tf_op jit(solution)/shard_map/ppermute | solution.py:14
  212.7 6.5 %concatenate.42 = f32[16,16384]{1,0:T(8,128)S(1)} concatenate(f32[4,16384]{1,0:T(4,128)S(1)} %reshape_reshape.42, f32[3,16384]{1,0:T(4,128)} %copy-done.38, f32[3,16384]{1,0:T(4,128)} %copy-done.41, f32[3,16384]{1,0:T(4,128)} %copy-done.44, f32[3,16384]{1,0:T(4,128)} %collective-permute-done.39), dimensions={0} | concatenate | bytes 2097152 | tf_op jit(solution)/shard_map/concatenate | solution.py:29
  230.3 6.7 %concatenate.36 = f32[16,16384]{1,0:T(8,128)S(1)} concatenate(f32[4,16384]{1,0:T(4,128)S(1)} %reshape_reshape.36, f32[3,16384]{1,0:T(4,128)} %collective-permute-done.12, f32[3,16384]{1,0:T(4,128)} %collective-permute-done.13, f32[3,16384]{1,0:T(4,128)} %collective-permute-done.14, f32[3,16384]{1,0:T(4,128)} %collective-permute-done.15), dimensions={0} | concatenate | bytes 2097152 | tf_op jit(solution)/shard_map/concatenate | solution.py:29
  251.9 5.1 collective-permute-start.16
  261.5 14.8 %collective-permute-start.19 = (f32[3,16384]{1,0:T(4,128)}, f32[3,16384]{1,0:T(4,128)}, u32[]{:S(2)}, u32[]{:S(2)}) collective-permute-start(f32[3,16384]{1,0:T(4,128)} %fusion.330), channel_id=1, source_target_pairs={{0,2},{1,3},{2,4},{3,5},{4,6},{5,7},{6,8},{7,9},{8,10},{9,11},{10,... | collective-permute-start | bytes 589832 | tf_op jit(solution)/shard_map/ppermute | solution.py:14
  276.4 6.2 %concatenate.43 = f32[16,16384]{1,0:T(8,128)S(1)} concatenate(f32[4,16384]{1,0:T(4,128)S(1)} %reshape_reshape.43, f32[3,16384]{1,0:T(4,128)} %copy-done.39, f32[3,16384]{1,0:T(4,128)} %copy-done.42, f32[3,16384]{1,0:T(4,128)} %copy-done.45, f32[3,16384]{1,0:T(4,128)} %collective-permute-done.43), dimensions={0} | concatenate | bytes 2097152 | tf_op jit(solution)/shard_map/concatenate | solution.py:29
  289.8 6.4 %concatenate.37 = f32[16,16384]{1,0:T(8,128)S(1)} concatenate(f32[4,16384]{1,0:T(4,128)S(1)} %reshape_reshape.37, f32[3,16384]{1,0:T(4,128)} %collective-permute-done.16, f32[3,16384]{1,0:T(4,128)} %collective-permute-done.17, f32[3,16384]{1,0:T(4,128)} %collective-permute-done.18, f32[3,16384]{1,0:T(4,128)} %collective-permute-done.19), dimensions={0} | concatenate | bytes 2097152 | tf_op jit(solution)/shard_map/concatenate | solution.py:29
  317.6 5.8 %collective-permute-done.21 = f32[3,16384]{1,0:T(4,128)S(1)} collective-permute-done((f32[3,16384]{1,0:T(4,128)}, f32[3,16384]{1,0:T(4,128)S(1)}, u32[]{:S(2)}, u32[]{:S(2)}) %collective-permute-start.21) | collective-permute-done | bytes 196640 | tf_op jit(solution)/shard_map/ppermute | solution.py:14
  324.8 6.2 %concatenate.38 = f32[16,16384]{1,0:T(8,128)S(1)} concatenate(f32[4,16384]{1,0:T(4,128)S(1)} %reshape_reshape.38, f32[3,16384]{1,0:T(4,128)} %copy-done.47, f32[3,16384]{1,0:T(4,128)} %copy-done.49, f32[3,16384]{1,0:T(4,128)} %copy-done.50, f32[3,16384]{1,0:T(4,128)} %collective-permute-done.23), dimensions={0} | concatenate | bytes 2097152 | tf_op jit(solution)/shard_map/concatenate | solution.py:29
  338.0 9.0 %stack.55 = f32[13,512,128]{1,0,2:T(8,128)} concatenate(f32[1,512,128]{1,0,2:T(1,128)S(1)} %copy-done.27, f32[1,512,128]{1,0,2:T(1,128)S(1)} %copy-done.30, f32[1,512,128]{1,0,2:T(1,128)S(1)} %copy-done.32, f32[1,512,128]{1,0,2:T(1,128)S(1)} %copy-done.34, f32[1,512,128]{1,0,2:T(1,128)S(1)} %copy-done.35, f32[1,512,128]{1,0,2:T(1,128)S(1)} %copy.74, f32[1,512,128]{1,0,2:T(1,128)S(1)} %copy.75, ...), dimensions={0} | concatenate | bytes 6815744 | tf_op jit(solution)/shard_map/stack | solution.py:95
  347.0 10.0 %fusion.499 = f32[128,13,13]{2,1,0:T(8,128)} fusion(f32[13,512,128]{1,0,2:T(8,128)} %stack.55), kind=kOutput, calls=%fused_computation.689 | convolution fusion | flops 132907008 | bytes 3494400 | tf_op jit(solution)/shard_map/arn,brn->nab/dot_general | solution.py:96
  357.2 134.9 %all-reduce.2.cloned.1.call-done = f32[128,13,13]{2,1,0:T(8,128)} async-done(((f32[128,13,13]{2,1,0:T(8,128)}), f32[128,13,13]{2,1,0:T(8,128)}) %all-reduce.2.cloned.1.call-update) | async-done | bytes 86544 | tf_op jit(solution)/shard_map/psum | solution.py:99
  (520 shorter events, 198.4 us)
Async XLA Ops:
  7.2 484.9 %all-reduce.2.cloned.1.call-start = ((), (), s32[]{:S(2)}) async-start(), calls=%async_computation | async-start | bytes 2097152 | tf_op jit(solution)/shard_map/psum | solution.py:99
  9.9 22.1 %collective-permute-start.24 = (f32[3,16384]{1,0:T(4,128)S(1)}, f32[3,16384]{1,0:T(4,128)S(1)}, u32[]{:S(2)}, u32[]{:S(2)}) collective-permute-start(f32[3,16384]{1,0:T(4,128)S(1)} %fusion.361), channel_id=1, source_target_pairs={{0,31},{1,0},{2,1},{3,2},{4,3},{5,4},{6,5},{7,6},{8,7},{9,8},{10,9... | collective-permute-start | bytes 589832 | tf_op jit(solution)/shard_map/ppermute | solution.py:14
  18.6 21.8 %collective-permute-start.27 = (f32[3,16384]{1,0:T(4,128)S(1)}, f32[3,16384]{1,0:T(4,128)}, u32[]{:S(2)}, u32[]{:S(2)}) collective-permute-start(f32[3,16384]{1,0:T(4,128)S(1)} %fusion.328), channel_id=1, source_target_pairs={{0,2},{1,3},{2,4},{3,5},{4,6},{5,7},{6,8},{7,9},{8,10},{9,11},{10,... | collective-permute-start | bytes 589832 | tf_op jit(solution)/shard_map/ppermute | solution.py:14
  21.1 32.2 %collective-permute-start = (f32[3,16384]{1,0:T(4,128)}, f32[3,16384]{1,0:T(4,128)}, u32[]{:S(2)}, u32[]{:S(2)}) collective-permute-start(f32[3,16384]{1,0:T(4,128)} %fusion.367), channel_id=1, source_target_pairs={{0,31},{1,0},{2,1},{3,2},{4,3},{5,4},{6,5},{7,6},{8,7},{9,8},{10,9... | collective-permute-start | bytes 589832 | tf_op jit(solution)/shard_map/ppermute | solution.py:14
  32.0 21.3 %collective-permute-start.1 = (f32[3,16384]{1,0:T(4,128)}, f32[3,16384]{1,0:T(4,128)}, u32[]{:S(2)}, u32[]{:S(2)}) collective-permute-start(f32[3,16384]{1,0:T(4,128)} %fusion.356), channel_id=1, source_target_pairs={{0,30},{1,31},{2,0},{3,1},{4,2},{5,3},{6,4},{7,5},{8,6},{9,7},{10,... | collective-permute-start | bytes 589832 | tf_op jit(solution)/shard_map/ppermute | solution.py:14
  71.7 24.5 %collective-permute-start.31 = (f32[3,16384]{1,0:T(4,128)S(1)}, f32[3,16384]{1,0:T(4,128)}, u32[]{:S(2)}, u32[]{:S(2)}) collective-permute-start(f32[3,16384]{1,0:T(4,128)S(1)} %copy-done.51), channel_id=1, source_target_pairs={{0,2},{1,3},{2,4},{3,5},{4,6},{5,7},{6,8},{7,9},{8,10},{9,11},{10,... | collective-permute-start | bytes 589832 | tf_op jit(solution)/shard_map/ppermute | solution.py:14
  73.6 39.5 %collective-permute-start.4 = (f32[3,16384]{1,0:T(4,128)}, f32[3,16384]{1,0:T(4,128)}, u32[]{:S(2)}, u32[]{:S(2)}) collective-permute-start(f32[3,16384]{1,0:T(4,128)} %fusion.366), channel_id=1, source_target_pairs={{0,31},{1,0},{2,1},{3,2},{4,3},{5,4},{6,5},{7,6},{8,7},{9,8},{10,9... | collective-permute-start | bytes 589832 | tf_op jit(solution)/shard_map/ppermute | solution.py:14
  81.7 31.4 %collective-permute-start.5 = (f32[3,16384]{1,0:T(4,128)}, f32[3,16384]{1,0:T(4,128)}, u32[]{:S(2)}, u32[]{:S(2)}) collective-permute-start(f32[3,16384]{1,0:T(4,128)} %fusion.355), channel_id=1, source_target_pairs={{0,30},{1,31},{2,0},{3,1},{4,2},{5,3},{6,4},{7,5},{8,6},{9,7},{10,... | collective-permute-start | bytes 589832 | tf_op jit(solution)/shard_map/ppermute | solution.py:14
  83.6 29.5 %collective-permute-start.6 = (f32[3,16384]{1,0:T(4,128)}, f32[3,16384]{1,0:T(4,128)}, u32[]{:S(2)}, u32[]{:S(2)}) collective-permute-start(f32[3,16384]{1,0:T(4,128)} %fusion.344), channel_id=1, source_target_pairs={{0,1},{1,2},{2,3},{3,4},{4,5},{5,6},{6,7},{7,8},{8,9},{9,10},{10,1... | collective-permute-start | bytes 589832 | tf_op jit(solution)/shard_map/ppermute | solution.py:14
  83.7 29.5 %collective-permute-start.7 = (f32[3,16384]{1,0:T(4,128)}, f32[3,16384]{1,0:T(4,128)}, u32[]{:S(2)}, u32[]{:S(2)}) collective-permute-start(f32[3,16384]{1,0:T(4,128)} %fusion.333), channel_id=1, source_target_pairs={{0,2},{1,3},{2,4},{3,5},{4,6},{5,7},{6,8},{7,9},{8,10},{9,11},{10,... | collective-permute-start | bytes 589832 | tf_op jit(solution)/shard_map/ppermute | solution.py:14
  132.9 23.6 %collective-permute-start.32 = (f32[3,16384]{1,0:T(4,128)S(1)}, f32[3,16384]{1,0:T(4,128)}, u32[]{:S(2)}, u32[]{:S(2)}) collective-permute-start(f32[3,16384]{1,0:T(4,128)S(1)} %fusion.359), channel_id=1, source_target_pairs={{0,31},{1,0},{2,1},{3,2},{4,3},{5,4},{6,5},{7,6},{8,7},{9,8},{10,9... | collective-permute-start | bytes 589832 | tf_op jit(solution)/shard_map/ppermute | solution.py:14
  137.5 33.3 %collective-permute-start.10 = (f32[3,16384]{1,0:T(4,128)}, f32[3,16384]{1,0:T(4,128)}, u32[]{:S(2)}, u32[]{:S(2)}) collective-permute-start(f32[3,16384]{1,0:T(4,128)} %fusion.343), channel_id=1, source_target_pairs={{0,1},{1,2},{2,3},{3,4},{4,5},{5,6},{6,7},{7,8},{8,9},{9,10},{10,1... | collective-permute-start | bytes 589832 | tf_op jit(solution)/shard_map/ppermute | solution.py:14
  138.9 32.0 %collective-permute-start.11 = (f32[3,16384]{1,0:T(4,128)}, f32[3,16384]{1,0:T(4,128)}, u32[]{:S(2)}, u32[]{:S(2)}) collective-permute-start(f32[3,16384]{1,0:T(4,128)} %fusion.332), channel_id=1, source_target_pairs={{0,2},{1,3},{2,4},{3,5},{4,6},{5,7},{6,8},{7,9},{8,10},{9,11},{10,... | collective-permute-start | bytes 589832 | tf_op jit(solution)/shard_map/ppermute | solution.py:14
  140.8 30.0 %collective-permute-start.9 = (f32[3,16384]{1,0:T(4,128)}, f32[3,16384]{1,0:T(4,128)}, u32[]{:S(2)}, u32[]{:S(2)}) collective-permute-start(f32[3,16384]{1,0:T(4,128)} %fusion.354), channel_id=1, source_target_pairs={{0,30},{1,31},{2,0},{3,1},{4,2},{5,3},{6,4},{7,5},{8,6},{9,7},{10,... | collective-permute-start | bytes 589832 | tf_op jit(solution)/shard_map/ppermute | solution.py:14
  191.7 20.9 %collective-permute-start.39 = (f32[3,16384]{1,0:T(4,128)}, f32[3,16384]{1,0:T(4,128)}, u32[]{:S(2)}, u32[]{:S(2)}) collective-permute-start(f32[3,16384]{1,0:T(4,128)} %fusion.325), channel_id=1, source_target_pairs={{0,2},{1,3},{2,4},{3,5},{4,6},{5,7},{6,8},{7,9},{8,10},{9,11},{10,... | collective-permute-start | bytes 589832 | tf_op jit(solution)/shard_map/ppermute | solution.py:14
  195.3 35.0 %collective-permute-start.12 = (f32[3,16384]{1,0:T(4,128)}, f32[3,16384]{1,0:T(4,128)}, u32[]{:S(2)}, u32[]{:S(2)}) collective-permute-start(f32[3,16384]{1,0:T(4,128)} %fusion.364), channel_id=1, source_target_pairs={{0,31},{1,0},{2,1},{3,2},{4,3},{5,4},{6,5},{7,6},{8,7},{9,8},{10,9... | collective-permute-start | bytes 589832 | tf_op jit(solution)/shard_map/ppermute | solution.py:14
  201.5 28.7 %collective-permute-start.13 = (f32[3,16384]{1,0:T(4,128)}, f32[3,16384]{1,0:T(4,128)}, u32[]{:S(2)}, u32[]{:S(2)}) collective-permute-start(f32[3,16384]{1,0:T(4,128)} %fusion.353), channel_id=1, source_target_pairs={{0,30},{1,31},{2,0},{3,1},{4,2},{5,3},{6,4},{7,5},{8,6},{9,7},{10,... | collective-permute-start | bytes 589832 | tf_op jit(solution)/shard_map/ppermute | solution.py:14
  206.1 24.2 %collective-permute-start.14 = (f32[3,16384]{1,0:T(4,128)}, f32[3,16384]{1,0:T(4,128)}, u32[]{:S(2)}, u32[]{:S(2)}) collective-permute-start(f32[3,16384]{1,0:T(4,128)} %fusion.342), channel_id=1, source_target_pairs={{0,1},{1,2},{2,3},{3,4},{4,5},{5,6},{6,7},{7,8},{8,9},{9,10},{10,1... | collective-permute-start | bytes 589832 | tf_op jit(solution)/shard_map/ppermute | solution.py:14
  206.1 24.2 %collective-permute-start.15 = (f32[3,16384]{1,0:T(4,128)}, f32[3,16384]{1,0:T(4,128)}, u32[]{:S(2)}, u32[]{:S(2)}) collective-permute-start(f32[3,16384]{1,0:T(4,128)} %fusion.331), channel_id=1, source_target_pairs={{0,2},{1,3},{2,4},{3,5},{4,6},{5,7},{6,8},{7,9},{8,10},{9,11},{10,... | collective-permute-start | bytes 589832 | tf_op jit(solution)/shard_map/ppermute | solution.py:14
  249.2 27.2 %collective-permute-start.43 = (f32[3,16384]{1,0:T(4,128)}, f32[3,16384]{1,0:T(4,128)}, u32[]{:S(2)}, u32[]{:S(2)}) collective-permute-start(f32[3,16384]{1,0:T(4,128)} %fusion.324), channel_id=1, source_target_pairs={{0,2},{1,3},{2,4},{3,5},{4,6},{5,7},{6,8},{7,9},{8,10},{9,11},{10,... | collective-permute-start | bytes 589832 | tf_op jit(solution)/shard_map/ppermute | solution.py:14
  251.9 37.8 %collective-permute-start.16 = (f32[3,16384]{1,0:T(4,128)}, f32[3,16384]{1,0:T(4,128)}, u32[]{:S(2)}, u32[]{:S(2)}) collective-permute-start(f32[3,16384]{1,0:T(4,128)} %fusion.363), channel_id=1, source_target_pairs={{0,31},{1,0},{2,1},{3,2},{4,3},{5,4},{6,5},{7,6},{8,7},{9,8},{10,9... | collective-permute-start | bytes 589832 | tf_op jit(solution)/shard_map/ppermute | solution.py:14
  259.1 30.7 %collective-permute-start.17 = (f32[3,16384]{1,0:T(4,128)}, f32[3,16384]{1,0:T(4,128)}, u32[]{:S(2)}, u32[]{:S(2)}) collective-permute-start(f32[3,16384]{1,0:T(4,128)} %fusion.352), channel_id=1, source_target_pairs={{0,30},{1,31},{2,0},{3,1},{4,2},{5,3},{6,4},{7,5},{8,6},{9,7},{10,... | collective-permute-start | bytes 589832 | tf_op jit(solution)/shard_map/ppermute | solution.py:14
  261.5 28.2 %collective-permute-start.18 = (f32[3,16384]{1,0:T(4,128)}, f32[3,16384]{1,0:T(4,128)}, u32[]{:S(2)}, u32[]{:S(2)}) collective-permute-start(f32[3,16384]{1,0:T(4,128)} %fusion.341), channel_id=1, source_target_pairs={{0,1},{1,2},{2,3},{3,4},{4,5},{5,6},{6,7},{7,8},{8,9},{9,10},{10,1... | collective-permute-start | bytes 589832 | tf_op jit(solution)/shard_map/ppermute | solution.py:14
  261.5 28.2 %collective-permute-start.19 = (f32[3,16384]{1,0:T(4,128)}, f32[3,16384]{1,0:T(4,128)}, u32[]{:S(2)}, u32[]{:S(2)}) collective-permute-start(f32[3,16384]{1,0:T(4,128)} %fusion.330), channel_id=1, source_target_pairs={{0,2},{1,3},{2,4},{3,5},{4,6},{5,7},{6,8},{7,9},{8,10},{9,11},{10,... | collective-permute-start | bytes 589832 | tf_op jit(solution)/shard_map/ppermute | solution.py:14
  (79 other events, 658.1 us)
Sparse Core Ops, SparseCore 0:
  357.2 134.8 all-reduce.1
where the time goes:
time: 523 us; the launch traced here: 516 us
  waiting for transfers between devices  151 us (29%)
  starting transfers between devices  119 us (23%)
  matrix products  117 us (22%)
  local copies, waits for them, and re-layouts  95.6 us (18%)
  other arithmetic  17 us (3%)
  between operations  16.7 us (3%)
    psum x1, waiting for transfers between devices, shards(): gram_matrix = lax.psum(local_gram, 'dom')  135 us
    ppermute x44, starting transfers between devices, from_behind(): lax.ppermute(shard, axis, [(i, (i + by) % peers) for i in range(peers)])  118 us
    concatenate x11, local copies, waits for them, and re-layouts, apply_blocks(): ghost_table = jnp.concatenate(pieces, axis=0)  63.5 us
    dot_general x44, matrix products, apply_blocks(): outgoing = jnp.dot(chooser, flat_rows, precision=highest)  44.7 us
    dot_general x66, matrix products, apply_blocks(): jnp.dot(chooser, ghost_table, precision=highest)  36.4 us
    dot_general x66, matrix products, apply_blocks(): jnp.einsum('icb,ibw->icw', block_vals[:, slot_index], picked, precision=h...  25.3 us
    another operation x14, local copies, waits for them, and re-layouts, shards(): basis_stack = jnp.stack(p_basis + r_basis)  18.5 us
    ppermute x44, waiting for transfers between devices, from_behind(): lax.ppermute(shard, axis, [(i, (i + by) % peers) for i in range(peers)])  16 us
  transfers between devices with their start and end apart: 45, of which 7 were waited for; matrix products, arithmetic and copies ran while one was open for 18% of the time, Pallas kernels for 0%

commit v1 on v0

--- a/solution.py
+++ b/solution.py
@@ -7,6 +7,14 @@
 BASIS = 13
 center_value = 4.5
 half_range = 4.5
+
+
+def add_in_pairs(x, mesh_axis):
+    n_dev, acc = (lax.axis_size(mesh_axis), x)
+    for far in [1 << k for k in range(n_dev.bit_length() - 1)]:
+        route = [(i, i ^ far) for i in range(n_dev)]
+        acc = acc + lax.ppermute(acc, mesh_axis, route)
+    return acc
 
 
 def from_behind(shard, axis, by):
@@ -96,7 +104,7 @@
     local_gram = jnp.einsum(
         "arn,brn->nab", basis_stack, basis_stack, precision=lax.Precision.HIGHEST
     )
-    gram_matrix = lax.psum(local_gram, "dom")
+    gram_matrix = add_in_pairs(local_gram, "dom")
     point_c, resid_c, direc_c = coefficient_steps(gram_matrix)
     highest = lax.Precision.HIGHEST
     new_point = start_point + jnp.einsum("na,arn->rn", point_c, basis_stack, precision=highest)

time: 523 us -> 422 us (0.81)
  waiting for transfers between devices: 151 us -> 30.2 us
  local copies, waits for them, and re-layouts: 95.6 us -> 109 us
  between operations: 16.7 us -> 3.4 us
  starting transfers between devices: 119 us -> 130 us
    psum x1 -> x0, waiting for transfers between devices: 135 us -> none  [shards(): gram_matrix = lax.psum(local_gram, 'dom')]
    ppermute x0 -> x5, waiting for transfers between devices: none -> 15.7 us  [add_in_pairs(): acc = acc + lax.ppermute(acc, mesh_axis, route)]
    ppermute x0 -> x5, starting transfers between devices: none -> 10.3 us  [add_in_pairs(): acc = acc + lax.ppermute(acc, mesh_axis, route)]
    ppermute x0 -> x5, local copies, waits for them, and re-layouts: none -> 7.02 us  [add_in_pairs(): acc = acc + lax.ppermute(acc, mesh_axis, route)]
    add x0 -> x4, other arithmetic: none -> 5.43 us  [add_in_pairs(): acc = acc + lax.ppermute(acc, mesh_axis, route)]
  transfers between devices with their start and end apart: 45 -> 49, of which waited for: 7 -> 12; matrix products, arithmetic and copies ran while one was open for 18% -> 23% of each run, Pallas kernels for 0% -> 0%
where the time goes in v1:
time: 422 us; the launch traced here: 414 us
  starting transfers between devices  130 us (31%)
  matrix products  119 us (28%)
  local copies, waits for them, and re-layouts  109 us (26%)
  waiting for transfers between devices  30.2 us (7%)
  other arithmetic  22 us (5%)
    ppermute x44, starting transfers between devices, from_behind(): lax.ppermute(shard, axis, [(i, (i + by) % peers) for i in range(peers)])  120 us
    concatenate x11, local copies, waits for them, and re-layouts, apply_blocks(): ghost_table = jnp.concatenate(pieces, axis=0)  62.8 us
    dot_general x44, matrix products, apply_blocks(): outgoing = jnp.dot(chooser, flat_rows, precision=highest)  47.6 us
    dot_general x66, matrix products, apply_blocks(): jnp.dot(chooser, ghost_table, precision=highest)  36.4 us
    dot_general x66, matrix products, apply_blocks(): jnp.einsum('icb,ibw->icw', block_vals[:, slot_index], picked, precision=h...  25.2 us
    another operation x14, local copies, waits for them, and re-layouts, shards(): basis_stack = jnp.stack(p_basis + r_basis)  21.9 us
    ppermute x5, waiting for transfers between devices, add_in_pairs(): acc = acc + lax.ppermute(acc, mesh_axis, route)  15.7 us
    ppermute x44, waiting for transfers between devices, from_behind(): lax.ppermute(shard, axis, [(i, (i + by) % peers) for i in range(peers)])  14.5 us
  transfers between devices with their start and end apart: 49, of which 12 were waited for; matrix products, arithmetic and copies ran while one was open for 23% of the time, Pallas kernels for 0%

profile of v1, /device:TPU:0, one launch (start us, length us, event | category | flops | bytes accessed | tf_op | source)
XLA Modules:
  0.0 414.2 jit_solution(8450069216115239414)
XLA Ops:
  4.1 6.4 %collective-permute-start.24 = (f32[3,16384]{1,0:T(4,128)}, f32[3,16384]{1,0:T(4,128)S(1)}, u32[]{:S(2)}, u32[]{:S(2)}) collective-permute-start(f32[3,16384]{1,0:T(4,128)} %fusion.361), channel_id=1, source_target_pairs={{0,31},{1,0},{2,1},{3,2},{4,3},{5,4},{6,5},{7,6},{8,7},{9,8},{10,9... | collective-permute-start | bytes 589832 | tf_op jit(solution)/shard_map/ppermute | solution.py:22
  15.2 5.1 %collective-permute-start = (f32[3,16384]{1,0:T(4,128)}, f32[3,16384]{1,0:T(4,128)}, u32[]{:S(2)}, u32[]{:S(2)}) collective-permute-start(f32[3,16384]{1,0:T(4,128)} %fusion.367), channel_id=1, source_target_pairs={{0,31},{1,0},{2,1},{3,2},{4,3},{5,4},{6,5},{7,6},{8,7},{9,8},{10,9... | collective-permute-start | bytes 589832 | tf_op jit(solution)/shard_map/ppermute | solution.py:22
  26.4 8.3 %collective-permute-start.3 = (f32[3,16384]{1,0:T(4,128)}, f32[3,16384]{1,0:T(4,128)}, u32[]{:S(2)}, u32[]{:S(2)}) collective-permute-start(f32[3,16384]{1,0:T(4,128)} %fusion.334), channel_id=1, source_target_pairs={{0,2},{1,3},{2,4},{3,5},{4,6},{5,7},{6,8},{7,9},{8,10},{9,11},{10,... | collective-permute-start | bytes 589832 | tf_op jit(solution)/shard_map/ppermute | solution.py:22
  47.5 6.5 %concatenate.33 = f32[16,16384]{1,0:T(8,128)S(1)} concatenate(f32[4,16384]{1,0:T(4,128)S(1)} %reshape_reshape.33, f32[3,16384]{1,0:T(4,128)} %collective-permute-done, f32[3,16384]{1,0:T(4,128)} %collective-permute-done.1, f32[3,16384]{1,0:T(4,128)} %collective-permute-done.2, f32[3,16384]{1,0:T(4,128)} %collective-permute-done.3), dimensions={0} | concatenate | bytes 2097152 | tf_op jit(solution)/shard_map/concatenate | solution.py:37
  68.4 5.1 %collective-permute-start.4 = (f32[3,16384]{1,0:T(4,128)}, f32[3,16384]{1,0:T(4,128)S(1)}, u32[]{:S(2)}, u32[]{:S(2)}) collective-permute-start(f32[3,16384]{1,0:T(4,128)} %fusion.366), channel_id=1, source_target_pairs={{0,31},{1,0},{2,1},{3,2},{4,3},{5,4},{6,5},{7,6},{8,7},{9,8},{10,9... | collective-permute-start | bytes 589832 | tf_op jit(solution)/shard_map/ppermute | solution.py:22
  78.5 12.7 %collective-permute-start.7 = (f32[3,16384]{1,0:T(4,128)}, f32[3,16384]{1,0:T(4,128)}, u32[]{:S(2)}, u32[]{:S(2)}) collective-permute-start(f32[3,16384]{1,0:T(4,128)} %fusion.333), channel_id=1, source_target_pairs={{0,2},{1,3},{2,4},{3,5},{4,6},{5,7},{6,8},{7,9},{8,10},{9,11},{10,... | collective-permute-start | bytes 589832 | tf_op jit(solution)/shard_map/ppermute | solution.py:22
  91.2 6.5 %concatenate.40 = f32[16,16384]{1,0:T(8,128)S(1)} concatenate(f32[4,16384]{1,0:T(4,128)S(1)} %reshape_reshape.40, f32[3,16384]{1,0:T(4,128)} %copy-done.35, f32[3,16384]{1,0:T(4,128)} %copy-done.38, f32[3,16384]{1,0:T(4,128)} %copy-done.41, f32[3,16384]{1,0:T(4,128)} %collective-permute-done.31), dimensions={0} | concatenate | bytes 2097152 | tf_op jit(solution)/shard_map/concatenate | solution.py:37
  109.5 6.7 %concatenate.34 = f32[16,16384]{1,0:T(8,128)S(1)} concatenate(f32[4,16384]{1,0:T(4,128)S(1)} %reshape_reshape.34, f32[3,16384]{1,0:T(4,128)} %copy-done.34, f32[3,16384]{1,0:T(4,128)} %collective-permute-done.5, f32[3,16384]{1,0:T(4,128)} %collective-permute-done.6, f32[3,16384]{1,0:T(4,128)} %collective-permute-done.7), dimensions={0} | concatenate | bytes 2097152 | tf_op jit(solution)/shard_map/concatenate | solution.py:37
  129.3 4.8 %collective-permute-start.32 = (f32[3,16384]{1,0:T(4,128)S(1)}, f32[3,16384]{1,0:T(4,128)}, u32[]{:S(2)}, u32[]{:S(2)}) collective-permute-start(f32[3,16384]{1,0:T(4,128)S(1)} %copy-done.49), channel_id=1, source_target_pairs={{0,31},{1,0},{2,1},{3,2},{4,3},{5,4},{6,5},{7,6},{8,7},{9,8},{10,9... | collective-permute-start | bytes 589832 | tf_op jit(solution)/shard_map/ppermute | solution.py:22
  137.0 10.4 %collective-permute-start.9 = (f32[3,16384]{1,0:T(4,128)}, f32[3,16384]{1,0:T(4,128)}, u32[]{:S(2)}, u32[]{:S(2)}) collective-permute-start(f32[3,16384]{1,0:T(4,128)} %fusion.354), channel_id=1, source_target_pairs={{0,30},{1,31},{2,0},{3,1},{4,2},{5,3},{6,4},{7,5},{8,6},{9,7},{10,... | collective-permute-start | bytes 589832 | tf_op jit(solution)/shard_map/ppermute | solution.py:22
  147.4 5.4 %collective-permute-start.8 = (f32[3,16384]{1,0:T(4,128)}, f32[3,16384]{1,0:T(4,128)}, u32[]{:S(2)}, u32[]{:S(2)}) collective-permute-start(f32[3,16384]{1,0:T(4,128)} %fusion.365), channel_id=1, source_target_pairs={{0,31},{1,0},{2,1},{3,2},{4,3},{5,4},{6,5},{7,6},{8,7},{9,8},{10,9... | collective-permute-start | bytes 589832 | tf_op jit(solution)/shard_map/ppermute | solution.py:22
  167.3 6.4 %concatenate.35 = f32[16,16384]{1,0:T(8,128)S(1)} concatenate(f32[4,16384]{1,0:T(4,128)S(1)} %reshape_reshape.35, f32[3,16384]{1,0:T(4,128)} %collective-permute-done.8, f32[3,16384]{1,0:T(4,128)} %collective-permute-done.9, f32[3,16384]{1,0:T(4,128)} %collective-permute-done.10, f32[3,16384]{1,0:T(4,128)} %collective-permute-done.11), dimensions={0} | concatenate | bytes 2097152 | tf_op jit(solution)/shard_map/concatenate | solution.py:37
  184.4 5.2 %collective-permute-start.37 = (f32[3,16384]{1,0:T(4,128)}, f32[3,16384]{1,0:T(4,128)S(1)}, u32[]{:S(2)}, u32[]{:S(2)}) collective-permute-start(f32[3,16384]{1,0:T(4,128)} %fusion.347), channel_id=1, source_target_pairs={{0,30},{1,31},{2,0},{3,1},{4,2},{5,3},{6,4},{7,5},{8,6},{9,7},{10,... | collective-permute-start | bytes 589832 | tf_op jit(solution)/shard_map/ppermute | solution.py:22
  202.5 6.8 %collective-permute-start.15 = (f32[3,16384]{1,0:T(4,128)}, f32[3,16384]{1,0:T(4,128)}, u32[]{:S(2)}, u32[]{:S(2)}) collective-permute-start(f32[3,16384]{1,0:T(4,128)} %fusion.331), channel_id=1, source_target_pairs={{0,2},{1,3},{2,4},{3,5},{4,6},{5,7},{6,8},{7,9},{8,10},{9,11},{10,... | collective-permute-start | bytes 589832 | tf_op jit(solution)/shard_map/ppermute | solution.py:22
  209.3 6.5 %concatenate.42 = f32[16,16384]{1,0:T(8,128)S(1)} concatenate(f32[4,16384]{1,0:T(4,128)S(1)} %reshape_reshape.42, f32[3,16384]{1,0:T(4,128)} %copy-done.36, f32[3,16384]{1,0:T(4,128)} %copy-done.39, f32[3,16384]{1,0:T(4,128)} %copy-done.42, f32[3,16384]{1,0:T(4,128)} %collective-permute-done.39), dimensions={0} | concatenate | bytes 2097152 | tf_op jit(solution)/shard_map/concatenate | solution.py:37
  226.9 6.7 %concatenate.36 = f32[16,16384]{1,0:T(8,128)S(1)} concatenate(f32[4,16384]{1,0:T(4,128)S(1)} %reshape_reshape.36, f32[3,16384]{1,0:T(4,128)} %collective-permute-done.12, f32[3,16384]{1,0:T(4,128)} %collective-permute-done.13, f32[3,16384]{1,0:T(4,128)} %collective-permute-done.14, f32[3,16384]{1,0:T(4,128)} %collective-permute-done.15), dimensions={0} | concatenate | bytes 2097152 | tf_op jit(solution)/shard_map/concatenate | solution.py:37
  248.6 5.1 %collective-permute-start.16 = (f32[3,16384]{1,0:T(4,128)}, f32[3,16384]{1,0:T(4,128)}, u32[]{:S(2)}, u32[]{:S(2)}) collective-permute-start(f32[3,16384]{1,0:T(4,128)} %fusion.363), channel_id=1, source_target_pairs={{0,31},{1,0},{2,1},{3,2},{4,3},{5,4},{6,5},{7,6},{8,7},{9,8},{10,9... | collective-permute-start | bytes 589832 | tf_op jit(solution)/shard_map/ppermute | solution.py:22
  259.1 13.5 %collective-permute-start.19 = (f32[3,16384]{1,0:T(4,128)}, f32[3,16384]{1,0:T(4,128)}, u32[]{:S(2)}, u32[]{:S(2)}) collective-permute-start(f32[3,16384]{1,0:T(4,128)} %fusion.330), channel_id=1, source_target_pairs={{0,2},{1,3},{2,4},{3,5},{4,6},{5,7},{6,8},{7,9},{8,10},{9,11},{10,... | collective-permute-start | bytes 589832 | tf_op jit(solution)/shard_map/ppermute | solution.py:22
  272.7 6.2 %concatenate.43 = f32[16,16384]{1,0:T(8,128)S(1)} concatenate(f32[4,16384]{1,0:T(4,128)S(1)} %reshape_reshape.43, f32[3,16384]{1,0:T(4,128)} %copy-done.37, f32[3,16384]{1,0:T(4,128)} %copy-done.40, f32[3,16384]{1,0:T(4,128)} %copy-done.43, f32[3,16384]{1,0:T(4,128)} %collective-permute-done.43), dimensions={0} | concatenate | bytes 2097152 | tf_op jit(solution)/shard_map/concatenate | solution.py:37
  286.1 6.4 %concatenate.37 = f32[16,16384]{1,0:T(8,128)S(1)} concatenate(f32[4,16384]{1,0:T(4,128)S(1)} %reshape_reshape.37, f32[3,16384]{1,0:T(4,128)} %collective-permute-done.16, f32[3,16384]{1,0:T(4,128)} %collective-permute-done.17, f32[3,16384]{1,0:T(4,128)} %collective-permute-done.18, f32[3,16384]{1,0:T(4,128)} %collective-permute-done.19), dimensions={0} | concatenate | bytes 2097152 | tf_op jit(solution)/shard_map/concatenate | solution.py:37
  314.6 5.8 %collective-permute-done.21 = f32[3,16384]{1,0:T(4,128)S(1)} collective-permute-done((f32[3,16384]{1,0:T(4,128)}, f32[3,16384]{1,0:T(4,128)S(1)}, u32[]{:S(2)}, u32[]{:S(2)}) %collective-permute-start.21) | collective-permute-done | bytes 196640 | tf_op jit(solution)/shard_map/ppermute | solution.py:22
  321.8 6.2 %concatenate.38 = f32[16,16384]{1,0:T(8,128)S(1)} concatenate(f32[4,16384]{1,0:T(4,128)S(1)} %reshape_reshape.38, f32[3,16384]{1,0:T(4,128)} %copy-done.45, f32[3,16384]{1,0:T(4,128)} %copy-done.47, f32[3,16384]{1,0:T(4,128)} %copy-done.48, f32[3,16384]{1,0:T(4,128)} %collective-permute-done.23), dimensions={0} | concatenate | bytes 2097152 | tf_op jit(solution)/shard_map/concatenate | solution.py:37
  334.9 11.8 %stack.55 = f32[13,512,128]{1,0,2:T(8,128)} concatenate(f32[1,512,128]{1,0,2:T(1,128)S(1)} %copy-done.25, f32[1,512,128]{1,0,2:T(1,128)S(1)} %copy-done.28, f32[1,512,128]{1,0,2:T(1,128)S(1)} %copy-done.30, f32[1,512,128]{1,0,2:T(1,128)S(1)} %copy-done.32, f32[1,512,128]{1,0,2:T(1,128)} %copy.113, f32[1,512,128]{1,0,2:T(1,128)S(1)} %copy.114, f32[1,512,128]{1,0,2:T(1,128)S(1)} %copy.115, ...), dimensions={0} | concatenate | bytes 6815744 | tf_op jit(solution)/shard_map/stack | solution.py:103
  346.7 9.0 %fusion.499 = f32[128,13,13]{2,1,0:T(8,128)S(1)} fusion(f32[13,512,128]{1,0,2:T(8,128)} %stack.55), kind=kOutput, calls=%fused_computation.689 | convolution fusion | flops 132907008 | bytes 3494400 | tf_op jit(solution)/shard_map/arn,brn->nab/dot_general | solution.py:104
  (531 shorter events, 237.6 us)
Async XLA Ops:
  4.1 21.8 %collective-permute-start.24 = (f32[3,16384]{1,0:T(4,128)}, f32[3,16384]{1,0:T(4,128)S(1)}, u32[]{:S(2)}, u32[]{:S(2)}) collective-permute-start(f32[3,16384]{1,0:T(4,128)} %fusion.361), channel_id=1, source_target_pairs={{0,31},{1,0},{2,1},{3,2},{4,3},{5,4},{6,5},{7,6},{8,7},{9,8},{10,9... | collective-permute-start | bytes 589832 | tf_op jit(solution)/shard_map/ppermute | solution.py:22
  12.6 22.0 %collective-permute-start.27 = (f32[3,16384]{1,0:T(4,128)S(1)}, f32[3,16384]{1,0:T(4,128)S(1)}, u32[]{:S(2)}, u32[]{:S(2)}) collective-permute-start(f32[3,16384]{1,0:T(4,128)S(1)} %fusion.328), channel_id=1, source_target_pairs={{0,2},{1,3},{2,4},{3,5},{4,6},{5,7},{6,8},{7,9},{8,10},{9,11},{10,... | collective-permute-start | bytes 589832 | tf_op jit(solution)/shard_map/ppermute | solution.py:22
  15.2 32.3 %collective-permute-start = (f32[3,16384]{1,0:T(4,128)}, f32[3,16384]{1,0:T(4,128)}, u32[]{:S(2)}, u32[]{:S(2)}) collective-permute-start(f32[3,16384]{1,0:T(4,128)} %fusion.367), channel_id=1, source_target_pairs={{0,31},{1,0},{2,1},{3,2},{4,3},{5,4},{6,5},{7,6},{8,7},{9,8},{10,9... | collective-permute-start | bytes 589832 | tf_op jit(solution)/shard_map/ppermute | solution.py:22
  25.9 21.7 %collective-permute-start.1 = (f32[3,16384]{1,0:T(4,128)}, f32[3,16384]{1,0:T(4,128)}, u32[]{:S(2)}, u32[]{:S(2)}) collective-permute-start(f32[3,16384]{1,0:T(4,128)} %fusion.356), channel_id=1, source_target_pairs={{0,30},{1,31},{2,0},{3,1},{4,2},{5,3},{6,4},{7,5},{8,6},{9,7},{10,... | collective-permute-start | bytes 589832 | tf_op jit(solution)/shard_map/ppermute | solution.py:22
  26.4 21.1 %collective-permute-start.2 = (f32[3,16384]{1,0:T(4,128)}, f32[3,16384]{1,0:T(4,128)}, u32[]{:S(2)}, u32[]{:S(2)}) collective-permute-start(f32[3,16384]{1,0:T(4,128)} %fusion.345), channel_id=1, source_target_pairs={{0,1},{1,2},{2,3},{3,4},{4,5},{5,6},{6,7},{7,8},{8,9},{9,10},{10,1... | collective-permute-start | bytes 589832 | tf_op jit(solution)/shard_map/ppermute | solution.py:22
  26.4 21.1 %collective-permute-start.3 = (f32[3,16384]{1,0:T(4,128)}, f32[3,16384]{1,0:T(4,128)}, u32[]{:S(2)}, u32[]{:S(2)}) collective-permute-start(f32[3,16384]{1,0:T(4,128)} %fusion.334), channel_id=1, source_target_pairs={{0,2},{1,3},{2,4},{3,5},{4,6},{5,7},{6,8},{7,9},{8,10},{9,11},{10,... | collective-permute-start | bytes 589832 | tf_op jit(solution)/shard_map/ppermute | solution.py:22
  66.5 24.7 %collective-permute-start.31 = (f32[3,16384]{1,0:T(4,128)}, f32[3,16384]{1,0:T(4,128)}, u32[]{:S(2)}, u32[]{:S(2)}) collective-permute-start(f32[3,16384]{1,0:T(4,128)} %fusion.327), channel_id=1, source_target_pairs={{0,2},{1,3},{2,4},{3,5},{4,6},{5,7},{6,8},{7,9},{8,10},{9,11},{10,... | collective-permute-start | bytes 589832 | tf_op jit(solution)/shard_map/ppermute | solution.py:22
  68.4 40.4 %collective-permute-start.4 = (f32[3,16384]{1,0:T(4,128)}, f32[3,16384]{1,0:T(4,128)S(1)}, u32[]{:S(2)}, u32[]{:S(2)}) collective-permute-start(f32[3,16384]{1,0:T(4,128)} %fusion.366), channel_id=1, source_target_pairs={{0,31},{1,0},{2,1},{3,2},{4,3},{5,4},{6,5},{7,6},{8,7},{9,8},{10,9... | collective-permute-start | bytes 589832 | tf_op jit(solution)/shard_map/ppermute | solution.py:22
  76.6 32.3 %collective-permute-start.5 = (f32[3,16384]{1,0:T(4,128)}, f32[3,16384]{1,0:T(4,128)}, u32[]{:S(2)}, u32[]{:S(2)}) collective-permute-start(f32[3,16384]{1,0:T(4,128)} %fusion.355), channel_id=1, source_target_pairs={{0,30},{1,31},{2,0},{3,1},{4,2},{5,3},{6,4},{7,5},{8,6},{9,7},{10,... | collective-permute-start | bytes 589832 | tf_op jit(solution)/shard_map/ppermute | solution.py:22
  78.5 30.3 %collective-permute-start.6 = (f32[3,16384]{1,0:T(4,128)}, f32[3,16384]{1,0:T(4,128)}, u32[]{:S(2)}, u32[]{:S(2)}) collective-permute-start(f32[3,16384]{1,0:T(4,128)} %fusion.344), channel_id=1, source_target_pairs={{0,1},{1,2},{2,3},{3,4},{4,5},{5,6},{6,7},{7,8},{8,9},{9,10},{10,1... | collective-permute-start | bytes 589832 | tf_op jit(solution)/shard_map/ppermute | solution.py:22
  78.5 31.0 %collective-permute-start.7 = (f32[3,16384]{1,0:T(4,128)}, f32[3,16384]{1,0:T(4,128)}, u32[]{:S(2)}, u32[]{:S(2)}) collective-permute-start(f32[3,16384]{1,0:T(4,128)} %fusion.333), channel_id=1, source_target_pairs={{0,2},{1,3},{2,4},{3,5},{4,6},{5,7},{6,8},{7,9},{8,10},{9,11},{10,... | collective-permute-start | bytes 589832 | tf_op jit(solution)/shard_map/ppermute | solution.py:22
  129.3 23.6 %collective-permute-start.32 = (f32[3,16384]{1,0:T(4,128)S(1)}, f32[3,16384]{1,0:T(4,128)}, u32[]{:S(2)}, u32[]{:S(2)}) collective-permute-start(f32[3,16384]{1,0:T(4,128)S(1)} %copy-done.49), channel_id=1, source_target_pairs={{0,31},{1,0},{2,1},{3,2},{4,3},{5,4},{6,5},{7,6},{8,7},{9,8},{10,9... | collective-permute-start | bytes 589832 | tf_op jit(solution)/shard_map/ppermute | solution.py:22
  134.1 33.2 %collective-permute-start.10 = (f32[3,16384]{1,0:T(4,128)}, f32[3,16384]{1,0:T(4,128)}, u32[]{:S(2)}, u32[]{:S(2)}) collective-permute-start(f32[3,16384]{1,0:T(4,128)} %fusion.343), channel_id=1, source_target_pairs={{0,1},{1,2},{2,3},{3,4},{4,5},{5,6},{6,7},{7,8},{8,9},{9,10},{10,1... | collective-permute-start | bytes 589832 | tf_op jit(solution)/shard_map/ppermute | solution.py:22
  135.3 32.0 %collective-permute-start.11 = (f32[3,16384]{1,0:T(4,128)}, f32[3,16384]{1,0:T(4,128)}, u32[]{:S(2)}, u32[]{:S(2)}) collective-permute-start(f32[3,16384]{1,0:T(4,128)} %fusion.332), channel_id=1, source_target_pairs={{0,2},{1,3},{2,4},{3,5},{4,6},{5,7},{6,8},{7,9},{8,10},{9,11},{10,... | collective-permute-start | bytes 589832 | tf_op jit(solution)/shard_map/ppermute | solution.py:22
  137.0 30.3 %collective-permute-start.9 = (f32[3,16384]{1,0:T(4,128)}, f32[3,16384]{1,0:T(4,128)}, u32[]{:S(2)}, u32[]{:S(2)}) collective-permute-start(f32[3,16384]{1,0:T(4,128)} %fusion.354), channel_id=1, source_target_pairs={{0,30},{1,31},{2,0},{3,1},{4,2},{5,3},{6,4},{7,5},{8,6},{9,7},{10,... | collective-permute-start | bytes 589832 | tf_op jit(solution)/shard_map/ppermute | solution.py:22
  191.7 35.2 %collective-permute-start.12 = (f32[3,16384]{1,0:T(4,128)}, f32[3,16384]{1,0:T(4,128)}, u32[]{:S(2)}, u32[]{:S(2)}) collective-permute-start(f32[3,16384]{1,0:T(4,128)} %fusion.364), channel_id=1, source_target_pairs={{0,31},{1,0},{2,1},{3,2},{4,3},{5,4},{6,5},{7,6},{8,7},{9,8},{10,9... | collective-permute-start | bytes 589832 | tf_op jit(solution)/shard_map/ppermute | solution.py:22
  198.0 28.9 %collective-permute-start.13 = (f32[3,16384]{1,0:T(4,128)}, f32[3,16384]{1,0:T(4,128)}, u32[]{:S(2)}, u32[]{:S(2)}) collective-permute-start(f32[3,16384]{1,0:T(4,128)} %fusion.353), channel_id=1, source_target_pairs={{0,30},{1,31},{2,0},{3,1},{4,2},{5,3},{6,4},{7,5},{8,6},{9,7},{10,... | collective-permute-start | bytes 589832 | tf_op jit(solution)/shard_map/ppermute | solution.py:22
  202.5 24.4 %collective-permute-start.14 = (f32[3,16384]{1,0:T(4,128)}, f32[3,16384]{1,0:T(4,128)}, u32[]{:S(2)}, u32[]{:S(2)}) collective-permute-start(f32[3,16384]{1,0:T(4,128)} %fusion.342), channel_id=1, source_target_pairs={{0,1},{1,2},{2,3},{3,4},{4,5},{5,6},{6,7},{7,8},{8,9},{9,10},{10,1... | collective-permute-start | bytes 589832 | tf_op jit(solution)/shard_map/ppermute | solution.py:22
  202.5 24.4 %collective-permute-start.15 = (f32[3,16384]{1,0:T(4,128)}, f32[3,16384]{1,0:T(4,128)}, u32[]{:S(2)}, u32[]{:S(2)}) collective-permute-start(f32[3,16384]{1,0:T(4,128)} %fusion.331), channel_id=1, source_target_pairs={{0,2},{1,3},{2,4},{3,5},{4,6},{5,7},{6,8},{7,9},{8,10},{9,11},{10,... | collective-permute-start | bytes 589832 | tf_op jit(solution)/shard_map/ppermute | solution.py:22
  245.7 27.0 %collective-permute-start.43 = (f32[3,16384]{1,0:T(4,128)}, f32[3,16384]{1,0:T(4,128)}, u32[]{:S(2)}, u32[]{:S(2)}) collective-permute-start(f32[3,16384]{1,0:T(4,128)} %fusion.324), channel_id=1, source_target_pairs={{0,2},{1,3},{2,4},{3,5},{4,6},{5,7},{6,8},{7,9},{8,10},{9,11},{10,... | collective-permute-start | bytes 589832 | tf_op jit(solution)/shard_map/ppermute | solution.py:22
  248.6 37.5 %collective-permute-start.16 = (f32[3,16384]{1,0:T(4,128)}, f32[3,16384]{1,0:T(4,128)}, u32[]{:S(2)}, u32[]{:S(2)}) collective-permute-start(f32[3,16384]{1,0:T(4,128)} %fusion.363), channel_id=1, source_target_pairs={{0,31},{1,0},{2,1},{3,2},{4,3},{5,4},{6,5},{7,6},{8,7},{9,8},{10,9... | collective-permute-start | bytes 589832 | tf_op jit(solution)/shard_map/ppermute | solution.py:22
  255.8 30.3 %collective-permute-start.17 = (f32[3,16384]{1,0:T(4,128)}, f32[3,16384]{1,0:T(4,128)}, u32[]{:S(2)}, u32[]{:S(2)}) collective-permute-start(f32[3,16384]{1,0:T(4,128)} %fusion.352), channel_id=1, source_target_pairs={{0,30},{1,31},{2,0},{3,1},{4,2},{5,3},{6,4},{7,5},{8,6},{9,7},{10,... | collective-permute-start | bytes 589832 | tf_op jit(solution)/shard_map/ppermute | solution.py:22
  259.1 26.9 %collective-permute-start.18 = (f32[3,16384]{1,0:T(4,128)}, f32[3,16384]{1,0:T(4,128)}, u32[]{:S(2)}, u32[]{:S(2)}) collective-permute-start(f32[3,16384]{1,0:T(4,128)} %fusion.341), channel_id=1, source_target_pairs={{0,1},{1,2},{2,3},{3,4},{4,5},{5,6},{6,7},{7,8},{8,9},{9,10},{10,1... | collective-permute-start | bytes 589832 | tf_op jit(solution)/shard_map/ppermute | solution.py:22
  259.1 26.9 %collective-permute-start.19 = (f32[3,16384]{1,0:T(4,128)}, f32[3,16384]{1,0:T(4,128)}, u32[]{:S(2)}, u32[]{:S(2)}) collective-permute-start(f32[3,16384]{1,0:T(4,128)} %fusion.330), channel_id=1, source_target_pairs={{0,2},{1,3},{2,4},{3,5},{4,6},{5,7},{6,8},{7,9},{8,10},{9,11},{10,... | collective-permute-start | bytes 589832 | tf_op jit(solution)/shard_map/ppermute | solution.py:22
  (78 other events, 639.1 us)
